TPU v7x, 8 devices: a whole 2x2x1 slice. The times are simulated.
8 devices in a mesh: dp: 2 (over z, y), tp: 4 (over x, core).
Axes of the slice: x: 2, y: 2, z: 1, core: 2. Of those that a mesh axis runs over, the one named last changes fastest.
Arguments:
- x: bfloat16 [16384, 2048], P(('dp', 'tp'))
- grad_y: bfloat16 [16384, 2048], P(('dp', 'tp'))
- ln_gain: float32 [2048], replicated
- positions: int32 [1024], replicated
- w_q: bfloat16 [2048, 2048], P('dp', 'tp')
- w_kv: bfloat16 [2048, 512], P('dp')
- w_o: bfloat16 [2048, 2048], P('tp', 'dp')
- w_in: bfloat16 [2, 2048, 16384], P(None, 'dp', 'tp')
- w_out: bfloat16 [16384, 2048], P('tp', 'dp')
Outputs:
- output 1: bfloat16 [16384, 2048], P(('dp', 'tp'))
- output 2: bfloat16 [16384, 2048], P(('dp', 'tp'))
- output 3: bfloat16 [2048, 2048], P('dp', 'tp')
- output 4: bfloat16 [2048, 512], P('dp')
- output 5: bfloat16 [2048, 2048], P('tp', 'dp')
- output 6: bfloat16 [2, 2048, 16384], P(None, 'dp', 'tp')
- output 7: bfloat16 [16384, 2048], P('tp', 'dp')
All inputs are finite; a program needn't handle non-finite values.
Results may differ from a plain program's by a relative error of at most 0.0126665.
Values are sent between devices in bfloat16 or wider.
A program may use at most 1 GiB of HBM per device.

v0:
```python
import functools
import jax
import jax.numpy as jnp
from jax import lax
from jax.sharding import PartitionSpec as P

LN_EPS = 1e-6
MASK_FILL = -1e30


def layer_norm(x_rows, ln_gain):
    x_wide = x_rows.astype(jnp.float32)
    centered = x_wide - jnp.mean(x_wide, axis=-1, keepdims=True)
    variance = jnp.mean(centered * centered, axis=-1, keepdims=True)
    return (centered * lax.rsqrt(variance + LN_EPS) * ln_gain).astype(jnp.bfloat16)


def swiglu(gate_up):
    return (jax.nn.silu(gate_up[0].astype(jnp.float32)) * gate_up[1].astype(jnp.float32)).astype(jnp.bfloat16)


def attention_forward(q_heads, key_seq, val_seq, visible, score_scale):
    scores = jnp.einsum("bqhe,bke->bhqk", q_heads, key_seq, preferred_element_type=jnp.float32) * score_scale
    scores = jnp.where(visible, scores, MASK_FILL)
    attn_prob = jax.nn.softmax(scores, axis=-1).astype(jnp.bfloat16)
    attn_out = jnp.einsum("bhqk,bke->bqhe", attn_prob, val_seq, preferred_element_type=jnp.float32)
    return attn_out.astype(jnp.bfloat16), attn_prob


def attention_backward(d_attn, q_heads, key_seq, val_seq, attn_prob, score_scale):
    d_prob = jnp.einsum("bqhe,bke->bhqk", d_attn, val_seq, preferred_element_type=jnp.float32)
    d_prob = d_prob.astype(jnp.bfloat16).astype(jnp.float32)
    prob_wide = attn_prob.astype(jnp.float32)
    row_dot = jnp.sum(prob_wide * d_prob, axis=-1, keepdims=True)
    d_scores = (prob_wide * (d_prob - row_dot) * score_scale).astype(jnp.bfloat16)
    d_query = jnp.einsum("bhqk,bke->bqhe", d_scores, key_seq, preferred_element_type=jnp.float32)
    d_key = jnp.einsum("bhqk,bqhe->bke", d_scores, q_heads, preferred_element_type=jnp.float32)
    d_val = jnp.einsum("bhqk,bqhe->bke", attn_prob, d_attn, preferred_element_type=jnp.float32)
    return d_query.astype(jnp.bfloat16), d_key, d_val


def solution(mesh):
    model_size = mesh.shape["tp"]
    row_spec = P(("dp", "tp"), None)
    weight_specs = (P("dp", "tp"), P("dp", None), P("tp", "dp"), P(None, "dp", "tp"), P("tp", "dp"))

    def device_body(x_rows, grad_rows, ln_gain, positions, wq_shard, wkv_shard, wo_shard, win_shard, wout_shard):
        head_dim = wkv_shard.shape[1] // 2
        local_heads = wq_shard.shape[1] // head_dim
        seq_len = positions.shape[0]
        tokens = x_rows.shape[0] * model_size
        num_seqs = tokens // seq_len
        score_scale = head_dim ** -0.5
        visible = positions[None, :] <= positions[:, None]

        w_q = lax.all_gather(wq_shard, "dp", axis=0, tiled=True)
        w_kv = lax.all_gather(wkv_shard, "dp", axis=0, tiled=True)
        w_o = lax.all_gather(wo_shard, "dp", axis=1, tiled=True)
        w_in = lax.all_gather(win_shard, "dp", axis=1, tiled=True)
        w_out = lax.all_gather(wout_shard, "dp", axis=1, tiled=True)

        normed_rows, norm_pullback = jax.vjp(functools.partial(layer_norm, ln_gain=ln_gain), x_rows)
        normed = lax.all_gather(normed_rows, "tp", axis=0, tiled=True)
        kv_rows = jnp.dot(normed_rows, w_kv, preferred_element_type=jnp.float32).astype(jnp.bfloat16)
        kv_all = lax.all_gather(kv_rows, "tp", axis=0, tiled=True).reshape(num_seqs, seq_len, 2 * head_dim)
        key_seq = kv_all[..., :head_dim]
        val_seq = kv_all[..., head_dim:]
        q_heads = jnp.dot(normed, w_q, preferred_element_type=jnp.float32).astype(jnp.bfloat16)
        q_heads = q_heads.reshape(num_seqs, seq_len, local_heads, head_dim)
        attn_out, attn_prob = attention_forward(q_heads, key_seq, val_seq, visible, score_scale)
        attn_flat = attn_out.reshape(tokens, local_heads * head_dim)
        gate_up = jnp.einsum("td,gdf->gtf", normed, w_in, preferred_element_type=jnp.float32).astype(jnp.bfloat16)
        mlp_act, act_pullback = jax.vjp(swiglu, gate_up)
        y_part = jnp.dot(attn_flat, w_o, preferred_element_type=jnp.float32) + jnp.dot(mlp_act, w_out, preferred_element_type=jnp.float32)
        y_rows = lax.psum_scatter(y_part, "tp", scatter_dimension=0, tiled=True).astype(jnp.bfloat16)

        grad_all = lax.all_gather(grad_rows, "tp", axis=0, tiled=True)
        d_act = jnp.einsum("td,fd->tf", grad_all, w_out, preferred_element_type=jnp.float32).astype(jnp.bfloat16)
        d_gate_up = act_pullback(d_act)[0]
        d_attn = jnp.einsum("td,ed->te", grad_all, w_o, preferred_element_type=jnp.float32).astype(jnp.bfloat16)
        d_query, d_key, d_val = attention_backward(d_attn.reshape(num_seqs, seq_len, local_heads, head_dim), q_heads, key_seq, val_seq, attn_prob, score_scale)
        d_query_flat = d_query.reshape(tokens, local_heads * head_dim)

        wout_part = jnp.einsum("tf,td->fd", mlp_act, grad_all, preferred_element_type=jnp.float32)
        wo_part = jnp.einsum("te,td->ed", attn_flat, grad_all, preferred_element_type=jnp.float32)
        win_part = jnp.einsum("td,gtf->gdf", normed, d_gate_up, preferred_element_type=jnp.float32)
        wq_part = jnp.einsum("td,te->de", normed, d_query_flat, preferred_element_type=jnp.float32)
        d_normed = jnp.einsum("te,de->td", d_query_flat, w_q, preferred_element_type=jnp.float32)
        d_normed = d_normed + jnp.einsum("gtf,gdf->td", d_gate_up, w_in, preferred_element_type=jnp.float32)

        d_kv = jnp.concatenate([d_key, d_val], axis=-1).reshape(tokens, 2 * head_dim)
        d_kv_rows = lax.psum_scatter(d_kv, "tp", scatter_dimension=0, tiled=True).astype(jnp.bfloat16)
        d_normed_rows = lax.psum_scatter(d_normed, "tp", scatter_dimension=0, tiled=True)
        d_normed_rows = d_normed_rows + jnp.einsum("tc,dc->td", d_kv_rows, w_kv, preferred_element_type=jnp.float32)
        wkv_part = jnp.einsum("td,tc->dc", normed_rows, d_kv_rows, preferred_element_type=jnp.float32)
        grad_x_rows = norm_pullback(d_normed_rows.astype(jnp.bfloat16))[0]

        grad_wq = lax.psum_scatter(wq_part, "dp", scatter_dimension=0, tiled=True).astype(jnp.bfloat16)
        wkv_scattered = lax.psum_scatter(wkv_part, "dp", scatter_dimension=0, tiled=True)
        grad_wkv = lax.psum(wkv_scattered, "tp").astype(jnp.bfloat16)
        grad_wo = lax.psum_scatter(wo_part, "dp", scatter_dimension=1, tiled=True).astype(jnp.bfloat16)
        grad_win = lax.psum_scatter(win_part, "dp", scatter_dimension=1, tiled=True).astype(jnp.bfloat16)
        grad_wout = lax.psum_scatter(wout_part, "dp", scatter_dimension=1, tiled=True).astype(jnp.bfloat16)
        return y_rows, grad_x_rows, grad_wq, grad_wkv, grad_wo, grad_win, grad_wout

    return jax.shard_map(device_body, mesh=mesh, in_specs=(row_spec, row_spec, P(None), P(None)) + weight_specs, out_specs=(row_spec, row_spec) + weight_specs, check_vma=False)
```

profile of v0, /device:TPU:0, one launch (start us, length us, event | category | flops | bytes accessed | tf_op | source)
XLA Modules:
  0.0 3630.2 jit_solution(10019772518458868244)
XLA Ops:
  7.2 0.7 all-gather.9.cloned.1.call-update
  8.0 0.7 all-gather.15.cloned.1.call-update
  8.7 4.7 convert_reduce_fusion
  13.4 5.8 fusion.32
  19.3 0.6 copy-done.7
  19.9 0.6 copy-done.3
  20.5 5.1 fusion.34
  25.6 0.5 all-gather.17.cloned.1.call-update
  26.2 0.5 all-gather.23.cloned.1.call-update
  26.8 15.7 all-gather.9.cloned.1.call-done
  42.5 9.8 convolution_convert_fusion.4
  52.4 0.7 all-gather.19.cloned.1.call-update
  53.1 0.7 all-gather.21.cloned.1.call-update
  53.9 0.7 broadcast_compare_fusion
  54.6 19.6 all-gather.15.cloned.1.call-done
  74.2 201.5 %all-gather.13.cloned.1.call-done = bf16[8192,2048]{1,0:T(8,128)(2,1)} async-done(((bf16[2048,2048]{1,0:T(8,128)(2,1)}), bf16[8192,2048]{1,0:T(8,128)(2,1)}) %all-gather.13.cloned.1.call-update) | async-done | bytes 33554448 | tf_op jit(solution)/shard_map/all_gather | solution.py:63
  275.7 24.5 convolution_convert_fusion.3
  300.1 12.5 reshape.67
  312.6 21.0 copy.54
  333.6 174.3 %all-gather.23.cloned.1.call-done = bf16[8192,2048]{1,0:T(8,128)(2,1)} async-done(((bf16[2048,2048]{1,0:T(8,128)(2,1)}), bf16[8192,2048]{1,0:T(8,128)(2,1)}) %all-gather.23.cloned.1.call-update) | async-done | bytes 33554448 | tf_op jit(solution)/shard_map/all_gather | solution.py:77
  508.0 24.4 convolution_convert_fusion.2
  532.4 12.5 reshape.69
  544.9 21.0 copy.56
  565.9 18.5 convolution_convert_fusion.1
  584.4 33.2 fusion.53
  617.6 32.8 divide_convert_fusion
  650.4 52.8 %fusion.39 = f32[8,1024,256]{1,2,0:T(8,128)} fusion(bf16[8,1024,2,256]{1,3,2,0:T(8,128)(2,1)} %copy.54, bf16[8,2,1024,1024]{2,3,1,0:T(8,128)(2,1)} %divide_convert_fusion, bf16[8,1024,1024,2]{2,1,3,0:T(8,128)(2,1)} %convolution_convert_fusion.1), kind=kOutput, calls=%fused_computation.71 | convolution fusion | flops 8740946944 | bytes 83886080 | tf_op jit(solution)/shard_map/bhqk,bqhe->bke/dot_general | solution.py:37
  703.2 19.3 convolution_bitcast_fusion
  722.6 12.0 pad_maximum_fusion
  734.6 16.4 copy.57
  751.1 49.3 %convert_bitcast_fusion.1 = bf16[8,1024,2,256]{1,3,2,0:T(8,128)(2,1)} fusion(bf16[8,2,1024,1024]{2,3,1,0:T(8,128)(2,1)} %divide_convert_fusion, bf16[8,1024,1024,2]{2,1,3,0:T(8,128)(2,1)} %convolution_convert_fusion.1, bf16[8,1024,512]{2,1,0:T(8,128)(2,1)} %bitcast.170), kind=kOutput, calls=%fused_computation.65 | convolution fusion | flops 8745141248 | bytes 146800640 | tf_op jit(solution)/shard_map/bhqk,bke->bqhe/dot_general | solution.py:36
  800.4 11.5 copy.52
  811.9 16.9 copy.78
  828.8 25.0 fusion.56
  853.9 18.6 convert_bitcast_fusion.2
  872.5 11.5 copy.48
  884.0 16.9 copy.77
  900.9 24.9 fusion.57
  925.8 26.3 all-gather.19.cloned.1.call-done
  952.2 292.0 %convert_bitcast_fusion = bf16[2,8192,4096]{2,1,0:T(8,128)(2,1)} fusion(bf16[2,2048,4096]{2,1,0:T(8,128)(2,1)} %all-gather.19.cloned.1.call-done, bf16[8192,2048]{1,0:T(8,128)(2,1)} %all-gather.13.cloned.1.call-done), kind=kOutput, calls=%fused_computation.18 | convolution fusion | flops 274945015808 | bytes 201326592 | tf_op jit(solution)/shard_map/td,gdf->gtf/dot_general | solution.py:72
  1244.1 227.5 %fusion.14 = (bf16[1,8192,4096]{2,1,0:T(8,128)(2,1)}, bf16[1,8192,4096]{2,1,0:T(8,128)(2,1)}, bf16[8192,4096]{1,0:T(8,128)(2,1)}) fusion(bf16[2,8192,4096]{2,1,0:T(8,128)(2,1)} %convert_bitcast_fusion, bf16[8192,2048]{1,0:T(8,128)(2,1)} %all-gather.23.cloned.1.call-done, bf16[4096,2048]{1,0:T(8,128)(2,1)} %all-gather.21.cloned.1.call-done), kind=kOutput, calls=%fused_computation.25 | convolution fusion | flops 138110042112 | bytes 385875968 | tf_op jit(solution)/shard_map/td,fd->tf/dot_general | solution.py:78
  1471.6 11.2 fusion.41
  1482.8 151.5 %fusion.58 = f32[4096,2048]{1,0:T(8,128)} fusion(bf16[8192,4096]{1,0:T(8,128)(2,1)} %get-tuple-element.30, bf16[8192,2048]{1,0:T(8,128)(2,1)} %all-gather.23.cloned.1.call-done), kind=kOutput, calls=%fused_computation.96 | convolution fusion | flops 137438953472 | bytes 134217728 | tf_op jit(solution)/shard_map/tf,td->fd/dot_general | solution.py:84
  1634.4 295.8 %fusion.25 = f32[2,2048,4096]{1,2,0:T(8,128)} fusion(bf16[8192,2048]{1,0:T(8,128)(2,1)} %all-gather.13.cloned.1.call-done, bf16[1,8192,4096]{2,1,0:T(8,128)(2,1)} %get-tuple-element.29, bf16[1,8192,4096]{2,1,0:T(8,128)(2,1)} %get-tuple-element.28), kind=kOutput, calls=%fused_computation.45 | convolution fusion | flops 274945015808 | bytes 234881024 | tf_op jit(solution)/shard_map/td,gtf->gdf/dot_general | solution.py:86
  1930.3 1.5 copy-done.11
  1931.8 29.9 fusion.55
  1961.7 322.8 %bitcast_add_fusion = f32[8192,2048]{1,0:T(8,128)} fusion(f32[8192,2048]{1,0:T(8,128)} %fusion.55, bf16[2,2048,4096]{2,1,0:T(8,128)(2,1)} %all-gather.19.cloned.1.call-done, bf16[1,8192,4096]{2,1,0:T(8,128)(2,1)} %get-tuple-element.29, bf16[1,8192,4096]{2,1,0:T(8,128)(2,1)} %get-tuple-element.28), kind=kOutput, calls=%fused_computation.28 | convolution fusion | flops 274961793024 | bytes 301989888 | tf_op jit(solution)/shard_map/gtf,gdf->td/dot_general | solution.py:89
  2284.6 1.5 copy-done.12
  2286.1 29.6 fusion.54
  2315.7 152.3 %convolution_add_fusion = f32[8192,2048]{1,0:T(8,128)} fusion(f32[8192,2048]{1,0:T(8,128)} %fusion.54, bf16[8192,4096]{1,0:T(8,128)(2,1)} %get-tuple-element.30, bf16[4096,2048]{1,0:T(8,128)(2,1)} %all-gather.21.cloned.1.call-done), kind=kOutput, calls=%fused_computation.37 | convolution fusion | flops 137455730688 | bytes 218103808 | tf_op jit(solution)/shard_map/dot_general | solution.py:74
  2468.1 2.7 convert_element_type.140
  2470.8 2.7 convert_element_type.142
  2473.5 42.3 %all-reduce.5 = bf16[1024,512]{1,0:T(8,128)(2,1)} all-reduce(f32[1024,512]{1,0:T(8,128)} %reduce-scatter.17.cloned.1.call-done), channel_id=1, replica_groups=mesh['dp'=2,'tp'=4] {'tp'}, use_global_device_ids=true, to_apply=%region_12.13 | all-reduce | flops 524288 | bytes 3145728 | tf_op jit(solution)/shard_map/psum | solution.py:100
  2515.8 9.1 convert_element_type.144
  2524.9 203.5 %reduce-scatter.21.cloned.1.call-done = f32[2,1024,4096]{1,2,0:T(8,128)} async-done(((f32[2,2048,4096]{1,2,0:T(8,128)}), f32[2,1024,4096]{1,2,0:T(8,128)}) %reduce-scatter.21.cloned.1.call-update) | async-done | bytes 33554448 | tf_op jit(solution)/shard_map/reduce_scatter | solution.py:102
  2728.4 17.5 convert_element_type.143
  2745.9 21.4 copy.60
  2767.3 404.1 %reduce-scatter.27.cloned.1.call-done = f32[2048,2048]{1,0:T(8,128)} async-done(((f32[8192,2048]{1,0:T(8,128)}), f32[2048,2048]{1,0:T(8,128)}) %reduce-scatter.27.cloned.1.call-update) | async-done | bytes 16777232
  3171.4 14.5 fusion.35
  3185.9 9.7 fusion.36
  3195.7 1.0 slice-done.3
  3196.7 7.6 add_convert_fusion
  3204.3 410.1 %reduce-scatter.25.cloned.1.call-done = f32[2048,2048]{1,0:T(8,128)} async-done(((f32[8192,2048]{1,0:T(8,128)}), f32[2048,2048]{1,0:T(8,128)}) %reduce-scatter.25.cloned.1.call-update) | async-done | bytes 16777232
  3614.3 9.0 convert_element_type.123
  (69 shorter events, 0.9 us)
Async XLA Ops:
  7.2 13.3 copy-start.5
  7.2 35.3 all-gather.9.cloned.1.call-start
  7.9 66.3 %all-gather.15.cloned.1.call-start = ((), (), s32[]{:S(2)}) async-start(), calls=%async_computation.11 | async-start | bytes 3145728 | tf_op jit(solution)/shard_map/all_gather | solution.py:56
  8.7 267.0 %all-gather.13.cloned.1.call-start = ((), (), s32[]{:S(2)}) async-start(), calls=%async_computation.10 | async-start | bytes 41943040 | tf_op jit(solution)/shard_map/all_gather | solution.py:63
  8.7 11.8 slice-start
  13.4 6.5 copy-start.1
  13.4 7.1 slice-start.1
  19.3 0.6 copy-start.7
  19.9 0.6 copy-start.3
  25.6 308.0 %all-gather.17.cloned.1.call-start = ((), (), s32[]{:S(2)}) async-start(), calls=%async_computation.12 | async-start | bytes 3145728 | tf_op jit(solution)/shard_map/all_gather | solution.py:58
  26.2 481.8 %all-gather.23.cloned.1.call-start = ((), (), s32[]{:S(2)}) async-start(), calls=%async_computation.15 | async-start | bytes 41943040 | tf_op jit(solution)/shard_map/all_gather | solution.py:77
  26.8 539.1 %all-gather.11.cloned.1.call-start = ((), (), s32[]{:S(2)}) async-start(), calls=%async_computation.9 | async-start | bytes 10485760 | tf_op jit(solution)/shard_map/all_gather | solution.py:65
  52.3 1.6 copy-start.9
  52.3 899.8 %all-gather.19.cloned.1.call-start = ((), (), s32[]{:S(2)}) async-start(), calls=%async_computation.13 | async-start | bytes 50331648 | tf_op jit(solution)/shard_map/all_gather | solution.py:59
  53.1 1191.0 %all-gather.21.cloned.1.call-start = ((), (), s32[]{:S(2)}) async-start(), calls=%async_computation.14 | async-start | bytes 25165824 | tf_op jit(solution)/shard_map/all_gather | solution.py:60
  53.8 1417.8 %reduce-scatter.13.cloned.1.call-start = ((), (), s32[]{:S(2)}) async-start(), calls=%async_computation.16 | async-start | bytes 20971520 | tf_op jit(solution)/shard_map/reduce_scatter | solution.py:92
  751.0 1717.0 %reduce-scatter.15.cloned.1.call-start = ((), (), s32[]{:S(2)}) async-start(), calls=%async_computation.17 | async-start | bytes 6291456 | tf_op jit(solution)/shard_map/reduce_scatter | solution.py:98
  853.8 1616.9 %reduce-scatter.19.cloned.1.call-start = ((), (), s32[]{:S(2)}) async-start(), calls=%async_computation.19 | async-start | bytes 6291456 | tf_op jit(solution)/shard_map/reduce_scatter | solution.py:101
  925.8 1547.7 %reduce-scatter.17.cloned.1.call-start = ((), (), s32[]{:S(2)}) async-start(), calls=%async_computation.18 | async-start | bytes 6291456 | tf_op jit(solution)/shard_map/reduce_scatter | solution.py:99
  1482.8 1033.0 %reduce-scatter.23.cloned.1.call-start = ((), (), s32[]{:S(2)}) async-start(), calls=%async_computation.21 | async-start | bytes 50331648 | tf_op jit(solution)/shard_map/reduce_scatter | solution.py:103
  1634.3 1094.1 %reduce-scatter.21.cloned.1.call-start = ((), (), s32[]{:S(2)}) async-start(), calls=%async_computation.20 | async-start | bytes 100663296 | tf_op jit(solution)/shard_map/reduce_scatter | solution.py:102
  1930.2 1.6 copy-start.11
  1930.2 1241.1 %reduce-scatter.27.cloned.1.call-start = ((), (), s32[]{:S(2)}) async-start(), calls=%async_computation.23 | async-start | bytes 83886080
  2284.5 1.6 copy-start.12
  2284.5 1329.8 %reduce-scatter.25.cloned.1.call-start = ((), (), s32[]{:S(2)}) async-start(), calls=%async_computation.22 | async-start | bytes 83886080
  2745.9 425.4 %copy-start.2 = (f32[2048]{0:T(1024)S(1)}, f32[2048]{0:T(1024)}, u32[]{:S(2)}) copy-start(f32[2048]{0:T(1024)} %copy-done.1) | copy-start | bytes 24580
  2745.9 425.4 %copy-start.6 = (f32[2048]{0:T(1024)S(1)}, f32[2048]{0:T(1024)}, u32[]{:S(2)}) copy-start(f32[2048]{0:T(1024)} %param.11) | copy-start | bytes 24580
  2745.9 425.4 %copy-start.10 = (bf16[2048,512]{1,0:T(8,128)(2,1)S(1)}, bf16[2048,512]{1,0:T(8,128)(2,1)}, u32[]{:S(2)}) copy-start(bf16[2048,512]{1,0:T(8,128)(2,1)} %all-gather.9.cloned.1.call-done) | copy-start | bytes 6291460
  2767.3 418.6 %copy-start.8 = (f32[2048]{0:T(1024)S(1)}, f32[2048]{0:T(1024)}, u32[]{:S(2)}) copy-start(f32[2048]{0:T(1024)} %copy-done.7) | copy-start | bytes 24580
  2767.3 418.6 %copy-start.4 = (f32[2048]{0:T(1024)S(1)}, f32[2048]{0:T(1024)}, u32[]{:S(2)}) copy-start(f32[2048]{0:T(1024)} %copy-done.3) | copy-start | bytes 24580
  3185.9 9.8 slice-start.2
  3185.9 9.8 copy-start
  3185.9 10.7 slice-start.3
Sparse Core Ops, SparseCore 0:
  9.5 32.9 all-gather.8
  44.0 30.1 all-gather.14
  76.3 199.3 all-gather.12
  277.0 30.1 all-gather.16
  308.6 199.3 all-gather.22
  509.3 55.7 all-gather.10
  566.6 385.4 all-gather.18
  953.7 196.6 all-gather.20
  1152.9 118.7 reduce-scatter.12
  1273.8 51.4 reduce-scatter.14
  1327.6 51.4 reduce-scatter.18
  1482.9 51.5 reduce-scatter.16
  1634.4 366.1 reduce-scatter.22
  2002.7 725.6 reduce-scatter.20
  2730.8 440.5 reduce-scatter.26
  3173.8 440.5 reduce-scatter.24
where the time goes:
time: 3640 us; the launch traced here: 3630 us
  matrix products  1830 us (50%)
  waiting for transfers between devices  1460 us (40%)
  local copies, waits for them, and re-layouts  167 us (5%)
  other arithmetic  119 us (3%)
  blocking collectives  42.3 us (1%)
    unnamed x18, waiting for transfers between devices  818 us
    dot_general x1, matrix products, device_body(): jnp.einsum('gtf,gdf->td', d_gate_up, w_in, preferred_element_type=jnp.flo...  323 us
    dot_general x1, matrix products, device_body(): jnp.einsum('td,gtf->gdf', normed, d_gate_up, preferred_element_type=jnp.f...  296 us
    dot_general x1, matrix products, device_body(): jnp.einsum('td,gdf->gtf', normed, w_in, preferred_element_type=jnp.float32)  292 us
    dot_general x1, matrix products, device_body(): jnp.einsum('td,fd->tf', grad_all, w_out, preferred_element_type=jnp.float32)  228 us
    reduce_scatter x1, waiting for transfers between devices, device_body(): lax.psum_scatter(win_part, 'dp', scatter_dimension=1, tiled=True)  204 us
    all_gather x1, waiting for transfers between devices, device_body(): normed = lax.all_gather(normed_rows, 'tp', axis=0, tiled=True)  201 us
    all_gather x1, waiting for transfers between devices, device_body(): grad_all = lax.all_gather(grad_rows, 'tp', axis=0, tiled=True)  174 us
  transfers between devices with their start and end apart: 16, of which 8 were waited for; matrix products, arithmetic and copies ran while one was open for 58% of the time, Pallas kernels for 0%

commit v1 on v0

v1 whole, which is shorter than its diff:
```python
import functools

import jax
import jax.numpy as jnp
from jax import lax
from jax.experimental import pallas as pl
from jax.experimental.pallas import tpu as pltpu
from jax.sharding import PartitionSpec as P


LN_EPS = 1e-6
MASK_FILL = -1e30
BF16 = jnp.bfloat16
F32 = jnp.float32
NN = (((1,), (0,)), ((), ()))
NT = (((1,), (1,)), ((), ()))
TN = (((0,), (0,)), ((), ()))
VMEM_LIMIT = 60 << 20
CHUNKS = 4


def mm(lhs, rhs, dims):
    return lax.dot_general(lhs, rhs, dims, preferred_element_type=F32)


def hidden(n):
    return [pl.BlockSpec(memory_space=pl.ANY)] * n


def params(n_axes):
    return pltpu.CompilerParams(dimension_semantics=("arbitrary",) * n_axes, vmem_limit_bytes=VMEM_LIMIT)


def norm_kernel(x_ref, gain_ref, h_ref):
    x = x_ref[...].astype(F32)
    c = x - jnp.mean(x, axis=-1, keepdims=True)
    var = jnp.mean(c * c, axis=-1, keepdims=True)
    h_ref[...] = (c * lax.rsqrt(var + LN_EPS) * gain_ref[...]).astype(BF16)


def norm_grad_kernel(x_ref, gain_ref, dh_ref, dx_ref):
    x = x_ref[...].astype(F32)
    c = x - jnp.mean(x, axis=-1, keepdims=True)
    rstd = lax.rsqrt(jnp.mean(c * c, axis=-1, keepdims=True) + LN_EPS)
    unit = c * rstd
    d = dh_ref[...].astype(F32) * gain_ref[...]
    d_mean = jnp.mean(d, axis=-1, keepdims=True)
    d_unit = jnp.mean(d * unit, axis=-1, keepdims=True)
    dx_ref[...] = (rstd * (d - d_mean - unit * d_unit)).astype(BF16)


def row_call(kernel, gain, *rows):
    tokens, width = rows[0].shape
    tm = min(256, tokens)
    block = pl.BlockSpec((tm, width), lambda m: (m, 0))
    return pl.pallas_call(
        kernel,
        grid=(tokens // tm,),
        in_specs=[block, pl.BlockSpec((1, width), lambda m: (0, 0))] + [block] * (len(rows) - 1),
        out_specs=block,
        out_shape=jax.ShapeDtypeStruct((tokens, width), BF16),
        compiler_params=params(1),
        cost_estimate=pl.CostEstimate(flops=16 * tokens * width, bytes_accessed=2 * tokens * width * (len(rows) + 1), transcendentals=tokens),
    )(rows[0], gain[None, :], *rows[1:])


def attention_kernel(scale, pos_q_ref, pos_k_ref, q_ref, key_ref, val_ref, do_ref, *rest):
    o_ref, dq_ref, dkv_ref = rest[-3:]
    head_dim = q_ref.shape[-1]
    visible = pos_k_ref[...] <= pos_q_ref[...]
    q, k, v, do = q_ref[...], key_ref[...], val_ref[...], do_ref[...]
    s = jnp.where(visible, mm(q, k, NT) * scale, MASK_FILL)
    e = jnp.exp(s - jnp.max(s, axis=-1, keepdims=True))
    p = (e / jnp.sum(e, axis=-1, keepdims=True)).astype(BF16)
    o_ref[...] = mm(p, v, NN).astype(BF16)
    dp = mm(do, v, NT).astype(BF16).astype(F32)
    pw = p.astype(F32)
    dot = jnp.sum(pw * dp, axis=-1, keepdims=True)
    ds = (pw * (dp - dot) * scale).astype(BF16)
    dq_ref[...] = mm(ds, k, NN).astype(BF16)

    @pl.when(pl.program_id(1) == 0)
    def _():
        dkv_ref[:, :head_dim] = mm(ds, q, TN)
        dkv_ref[:, head_dim:] = mm(p, do, TN)

    @pl.when(pl.program_id(1) > 0)
    def _():
        dkv_ref[:, :head_dim] += mm(ds, q, TN)
        dkv_ref[:, head_dim:] += mm(p, do, TN)


def attention(q, kv, do, positions, head_dim, after=()):
    tokens, width = q.shape
    seq = positions.shape[0]
    heads = width // head_dim
    block = lambda f: pl.BlockSpec((seq, head_dim), f)
    return pl.pallas_call(
        functools.partial(attention_kernel, head_dim ** -0.5),
        grid=(tokens // seq, heads),
        in_specs=[
            pl.BlockSpec((seq, 1), lambda s, h: (0, 0)),
            pl.BlockSpec((1, seq), lambda s, h: (0, 0)),
            block(lambda s, h: (s, h)),
            block(lambda s, h: (s, 0)),
            block(lambda s, h: (s, 1)),
            block(lambda s, h: (s, h)),
        ] + hidden(len(after)),
        out_specs=[block(lambda s, h: (s, h)), block(lambda s, h: (s, h)), pl.BlockSpec((seq, 2 * head_dim), lambda s, h: (s, 0))],
        out_shape=[
            jax.ShapeDtypeStruct((tokens, width), BF16),
            jax.ShapeDtypeStruct((tokens, width), BF16),
            jax.ShapeDtypeStruct((tokens, 2 * head_dim), F32),
        ],
        compiler_params=params(2),
        cost_estimate=pl.CostEstimate(flops=20 * tokens * seq * width, bytes_accessed=tokens * width * 14, transcendentals=tokens * seq * heads),
        name="attention",
    )(positions[:, None], positions[None, :], q, kv, kv, do, *after)


def mlp_kernel(sub, h_ref, gy_ref, win_ref, wout_ref, *rest):
    a_ref, dg_ref, du_ref = rest[-3:]
    for c in range(0, a_ref.shape[-1], sub):
        cols = slice(c, c + sub)
        g = mm(h_ref[...], win_ref[0, :, cols], NN).astype(BF16).astype(F32)
        u = mm(h_ref[...], win_ref[1, :, cols], NN).astype(BF16).astype(F32)
        d = mm(gy_ref[...], wout_ref[cols, :], NT).astype(BF16).astype(F32)
        sig = jax.nn.sigmoid(g)
        silu = g * sig
        a_ref[:, cols] = (silu * u).astype(BF16)
        du_ref[:, cols] = (d * silu).astype(BF16)
        dg_ref[:, cols] = (d * u * (sig + silu * (1.0 - sig))).astype(BF16)


def mlp_chunk(h, gy, win, wout, after=()):
    tokens, d_model = h.shape
    cols = wout.shape[0]
    tm, tn = min(512, tokens), min(512, cols)
    out_block = pl.BlockSpec((tm, tn), lambda n, m: (m, n))
    return pl.pallas_call(
        functools.partial(mlp_kernel, min(256, tn)),
        grid=(cols // tn, tokens // tm),
        in_specs=[
            pl.BlockSpec((tm, d_model), lambda n, m: (m, 0)),
            pl.BlockSpec((tm, d_model), lambda n, m: (m, 0)),
            pl.BlockSpec((2, d_model, tn), lambda n, m: (0, 0, n)),
            pl.BlockSpec((tn, d_model), lambda n, m: (n, 0)),
        ] + hidden(len(after)),
        out_specs=[out_block] * 3,
        out_shape=[jax.ShapeDtypeStruct((tokens, cols), BF16)] * 3,
        compiler_params=params(2),
        cost_estimate=pl.CostEstimate(flops=6 * tokens * d_model * cols, bytes_accessed=4 * tokens * d_model * (cols // tn) + 6 * tokens * cols, transcendentals=tokens * cols),
        name="mlp_chunk",
    )(h, gy, win, wout, *after)


def sum_kernel(terms, n_in, n_adds, out_dtype, *refs):
    out_ref = refs[-1]
    acc = None
    for lhs, rhs, pick, dims in terms:
        right = refs[rhs][...] if pick is None else refs[rhs][pick]
        part = mm(refs[lhs][...], right, dims)
        acc = part if acc is None else acc + part
    for i in range(n_in, n_in + n_adds):
        acc = acc + refs[i][...]
    out_ref[...] = acc.astype(out_dtype)


def sum_rows(products, adds, row0, rows, width, out_dtype, tm, tn, after=()):
    tm, tn = min(tm, rows), min(tn, width)
    base = row0 // tm
    arrays, specs, terms = [], [], []
    k_total = 0
    for lhs, rhs, form in products:
        left = lhs if isinstance(lhs, tuple) else (lhs,)
        first = len(arrays)
        for part in left:
            arrays.append(part)
            offset = base if part.shape[0] > rows else 0
            specs.append(pl.BlockSpec((tm, part.shape[1]), lambda n, m, o=offset: (o + m, 0)))
            k_total += part.shape[1]
        at = len(arrays)
        arrays.append(rhs)
        if form == "n":
            specs.append(pl.BlockSpec((rhs.shape[0], tn), lambda n, m: (0, n)))
        elif rhs.ndim == 2:
            specs.append(pl.BlockSpec((tn, rhs.shape[1]), lambda n, m: (n, 0)))
        else:
            specs.append(pl.BlockSpec((rhs.shape[0], tn, rhs.shape[2]), lambda n, m: (0, n, 0)))
        for i in range(len(left)):
            terms.append((first + i, at, i if rhs.ndim == 3 else None, NN if form == "n" else NT))
    n_in = len(arrays)
    for add in adds:
        arrays.append(add)
        specs.append(pl.BlockSpec((tm, tn), lambda n, m: (m, n)))
    return pl.pallas_call(
        functools.partial(sum_kernel, tuple(terms), n_in, len(adds), out_dtype),
        grid=(width // tn, rows // tm),
        in_specs=specs + hidden(len(after)),
        out_specs=pl.BlockSpec((tm, tn), lambda n, m: (m, n)),
        out_shape=jax.ShapeDtypeStruct((rows, width), out_dtype),
        compiler_params=params(2),
        cost_estimate=pl.CostEstimate(flops=2 * rows * width * k_total, bytes_accessed=2 * rows * k_total * (width // tn) + 2 * width * k_total + 4 * rows * width * (1 + len(adds)), transcendentals=0),
    )(*arrays, *after)


def pair_kernel(half, first_ref, second_ref, *rest):
    out_ref = rest[-1]

    @pl.when(pl.program_id(0) < half)
    def _():
        out_ref[...] = first_ref[...]

    @pl.when(pl.program_id(0) >= half)
    def _():
        out_ref[...] = second_ref[...]


def pair(first, second, after=()):
    tokens, width = first.shape
    tm = min(512, tokens)
    half = tokens // tm
    return pl.pallas_call(
        functools.partial(pair_kernel, half),
        grid=(2 * half,),
        in_specs=[
            pl.BlockSpec((tm, width), lambda m: (jnp.minimum(m, half - 1), 0)),
            pl.BlockSpec((tm, width), lambda m: (jnp.maximum(m - half, 0), 0)),
        ] + hidden(len(after)),
        out_specs=pl.BlockSpec((tm, width), lambda m: (m, 0)),
        out_shape=jax.ShapeDtypeStruct((2 * tokens, width), first.dtype),
        compiler_params=params(1),
        cost_estimate=pl.CostEstimate(flops=tokens * width, bytes_accessed=8 * tokens * width, transcendentals=0),
        name="pair",
    )(first, second, *after)


def place_kernel(piece_ref, *rest):
    rest[-1][...] = piece_ref[...].astype(BF16)


def place(piece, buffer, shape, index):
    dims = piece.shape
    rows = min(256, dims[0])
    lead = (1,) * (len(shape) - 2)
    at = lambda m: index[:-2] + (index[-2] * (dims[0] // rows) + m, index[-1])
    carried = () if buffer is None else (buffer,)
    return pl.pallas_call(
        place_kernel,
        grid=(dims[0] // rows,),
        in_specs=[pl.BlockSpec((rows, dims[1]), lambda m: (m, 0))] + hidden(len(carried)),
        out_specs=pl.BlockSpec((None,) * len(lead) + (rows, dims[1]), at),
        out_shape=jax.ShapeDtypeStruct(shape, BF16),
        input_output_aliases={1: 0} if carried else {},
        compiler_params=params(1),
        cost_estimate=pl.CostEstimate(flops=dims[0] * dims[1], bytes_accessed=6 * dims[0] * dims[1], transcendentals=0),
        name="place",
    )(piece, *carried)


def solution(mesh):
    tp = mesh.shape["tp"]
    row_spec = P(("dp", "tp"), None)
    weight_specs = (P("dp", "tp"), P("dp", None), P("tp", "dp"), P(None, "dp", "tp"), P("tp", "dp"))
    core_pairs = [(i, i ^ 1) for i in range(tp)]
    chip_pairs = [(i, i ^ 2) for i in range(tp)]

    def core(v):
        return lax.ppermute(v, "tp", core_pairs)

    def across(v):
        return lax.ppermute(v, "tp", chip_pairs)

    def tied(v, after):
        return lax.optimization_barrier((v, after))[0]

    def device_body(x_rows, gy_rows, ln_gain, positions, wq_shard, wkv_shard, wo_shard, win_shard, wout_shard):
        head_dim = wkv_shard.shape[1] // 2
        block, d_model = x_rows.shape
        ff = wout_shard.shape[0]
        step = ff // CHUNKS
        tp_index = lax.axis_index("tp")
        on_core, on_chip = tp_index % 2, tp_index // 2

        normed = row_call(norm_kernel, ln_gain, x_rows)
        h_across = across(normed)
        gy_across = across(gy_rows)
        h_near = pair(normed, core(normed))
        gy_near = pair(gy_rows, core(gy_rows))

        w_kv = lax.all_gather(wkv_shard, "dp", axis=0, tiled=True)
        w_q = lax.all_gather(wq_shard, "dp", axis=0, tiled=True)
        w_o = lax.all_gather(wo_shard, "dp", axis=1, tiled=True)
        win_late, wout_late = tied((win_shard, wout_shard), normed)
        w_in, w_out = [], []
        for j in range(CHUNKS):
            w_in.append(lax.all_gather(win_late[:, :, j * step:(j + 1) * step], "dp", axis=1, tiled=True))
            w_out.append(lax.all_gather(wout_late[j * step:(j + 1) * step], "dp", axis=1, tiled=True))

        def attend(h, gy):
            kv = mm(h, w_kv, NN).astype(BF16)
            q = mm(h, w_q, NN).astype(BF16)
            do = mm(gy, w_o, NT).astype(BF16)
            return attention(q, kv, do, positions, head_dim)

        o_near, dq_near, dkv_near = attend(h_near, gy_near)
        acts_near = [mlp_chunk(h_near, gy_near, w_in[0], w_out[0], after=(o_near,))]
        h_far = pair(h_across, core(h_across), after=(acts_near[0][0],))
        gy_far = pair(gy_across, core(gy_across), after=(acts_near[0][0],))
        o_far, dq_far, dkv_far = attend(h_far, gy_far)
        acts_far = [mlp_chunk(h_far, gy_far, w_in[0], w_out[0], after=(o_far,))]
        last = acts_far[0][0]

        from_core = core(dkv_near[block:]), core(dkv_far[block:])
        dkv_own = dkv_near[:block] + from_core[0]
        dkv_other = dkv_far[:block] + from_core[1]
        dkv_from = across(dkv_other)
        d_kv = (dkv_own + dkv_from).astype(BF16)

        def weight_grad(left, right, axis, last):
            parts = [mm(tied(left[i], last), right[i], TN) for i in range(2)]
            part = parts[0] + parts[1]
            return part, lax.psum_scatter(part, "dp", scatter_dimension=axis, tiled=True)

        h_both, gy_both = (h_near, h_far), (gy_near, gy_far)
        grad_out, grad_in = [None] * CHUNKS, [[None] * CHUNKS, [None] * CHUNKS]

        def do_out(j, last):
            part, grad_out[j] = weight_grad((acts_near[j][0], acts_far[j][0]), gy_both, 1, last)
            return part

        def do_in(j, last):
            for g in range(2):
                last, grad_in[g][j] = weight_grad(h_both, (acts_near[j][1 + g], acts_far[j][1 + g]), 0, last)
            return last

        def do_act(j, last):
            acts_near.append(mlp_chunk(h_near, gy_near, w_in[j], w_out[j], after=(last,)))
            acts_far.append(mlp_chunk(h_far, gy_far, w_in[j], w_out[j], after=(acts_near[-1][0],)))
            return acts_far[-1][0]

        def y_rows(near, row0, adds, dtype, last):
            acts, o = (acts_near, o_near) if near else (acts_far, o_far)
            products = [(acts[j][0], w_out[j], "n") for j in range(CHUNKS)] + [(o, w_o, "n")]
            return sum_rows(products, adds, row0, block, d_model, dtype, 512, 1024, after=(last,))

        def dh_rows(near, row0, adds, dtype, last, more=()):
            acts, dq = (acts_near, dq_near) if near else (acts_far, dq_far)
            products = [((acts[j][1], acts[j][2]), w_in[j], "t") for j in range(CHUNKS)] + [(dq, w_q, "t"), *more]
            return sum_rows(products, adds, row0, block, d_model, dtype, 512, 512, after=(last,))

        last, grad_wq = weight_grad(h_both, (dq_near, dq_far), 0, last)
        last, grad_wo = weight_grad((o_near, o_far), gy_both, 1, last)
        last = do_out(0, last)

        pick = lambda v, at: lax.dynamic_slice_in_dim(v, at * (v.shape[1] // 2), v.shape[1] // 2, axis=1)
        last = wkv_part = mm(tied(normed, last), d_kv, TN)
        wkv_part = pick(wkv_part, on_core) + core(pick(wkv_part, 1 - on_core))
        wkv_part = pick(wkv_part, on_chip) + across(pick(wkv_part, 1 - on_chip))
        last = do_in(0, last)
        last = do_act(1, last)
        last = do_out(1, last)
        last = do_act(2, last)
        last = do_in(1, last)
        last = do_act(3, last)
        y_diag = y_rows(False, block, (), F32, last)
        y_diag_from = core(y_diag)
        last = do_out(2, y_diag)
        grad_wkv = lax.psum_scatter(tied(wkv_part, last), "dp", scatter_dimension=0, tiled=True).astype(BF16)
        for exchange, side in ((across, on_chip), (core, on_core)):
            other = exchange(grad_wkv)
            grad_wkv = jnp.where(side == 0, jnp.concatenate([grad_wkv, other], axis=1), jnp.concatenate([other, grad_wkv], axis=1))

        y_across = y_rows(False, 0, (y_diag_from,), F32, last)
        y_from = across(y_across)
        last = do_in(2, y_across)
        dh_diag = dh_rows(False, block, (), F32, last)
        dh_diag_from = core(dh_diag)
        last = do_out(3, dh_diag)
        dh_across = dh_rows(False, 0, (dh_diag_from,), F32, last)
        dh_from = across(dh_across)
        last = do_in(3, dh_across)
        y_core = y_rows(True, block, (), F32, last)
        y_core_from = core(y_core)
        dh_core = dh_rows(True, block, (), F32, y_core)
        dh_core_from = core(dh_core)
        y_own = y_rows(True, 0, (y_core_from, y_from), BF16, dh_core)
        dh_own = dh_rows(True, 0, (dh_core_from, dh_from), BF16, y_own, more=((d_kv, w_kv, "t"),))
        grad_x = row_call(norm_grad_kernel, ln_gain, x_rows, dh_own)

        win_grad = wout_grad = None
        for j in range(CHUNKS):
            wout_grad = place(grad_out[j], wout_grad, wout_shard.shape, (j, 0))
            for g in range(2):
                win_grad = place(grad_in[g][j], win_grad, win_shard.shape, (g, 0, j))
        return y_own, grad_x, grad_wq.astype(BF16), grad_wkv, grad_wo.astype(BF16), win_grad, wout_grad

    return jax.shard_map(device_body, mesh=mesh, in_specs=(row_spec, row_spec, P(None), P(None)) + weight_specs, out_specs=(row_spec, row_spec) + weight_specs, check_vma=False)
```

time: 3640 us -> 2950 us (0.81)
  Pallas kernels: 0 us -> 1320 us
  matrix products: 1830 us -> 710 us
  waiting for transfers between devices: 1460 us -> 830 us
  local copies, waits for them, and re-layouts: 167 us -> 31.2 us
  other arithmetic: 119 us -> 23.4 us
  blocking collectives: 42.3 us -> 0 us
    pallas_call x0 -> x36, Pallas kernels: none -> 1320 us  [the longest x8 573 us: sum_rows(): pl.pallas_call(functools.partial(sum_kernel, tuple(terms), n_in, len(adds...]
    dot_general x20 -> x35, matrix products: 1790 us -> 710 us  [mm(): return lax.dot_general(lhs, rhs, dims, preferred_element_type=F32)]
    unnamed x18 -> x26, waiting for transfers between devices: 818 us -> 10.5 us
    ppermute x0 -> x19, waiting for transfers between devices: none -> 697 us  [the longest x7 672 us: across(): return lax.ppermute(v, 'tp', chip_pairs)]
    all_gather x5 -> x8, waiting for transfers between devices: 402 us -> 0.01 us  [the longest x4 0.01 us: device_body(): lax.all_gather(wout_late[j * step:(j + 1) * step], 'dp', axis=1, tiled=True)]
    reduce_scatter x6 -> x15, waiting for transfers between devices: 204 us -> 123 us  [the longest x14 123 us: weight_grad(): lax.psum_scatter(part, 'dp', scatter_dimension=axis, tiled=True)]
    convert_element_type x8 -> x4, other arithmetic: 86.5 us -> 12.6 us  [the longest x1 6.09 us: device_body(): d_kv = (dkv_own + dkv_from).astype(BF16)]
    reshape x4 -> x0, local copies, waits for them, and re-layouts: 67 us -> none  [the longest x2 33.5 us: device_body(): q_heads = q_heads.reshape(num_seqs, seq_len, local_heads, head_dim)]
  transfers between devices with their start and end apart: 16 -> 45, of which waited for: 8 -> 8; matrix products, arithmetic and copies ran while one was open for 58% -> 26% of each run, Pallas kernels for 0% -> 39%
where the time goes in v1:
time: 2950 us; the launch traced here: 2940 us
  Pallas kernels  1320 us (45%)
  waiting for transfers between devices  830 us (28%)
  matrix products  710 us (24%)
  local copies, waits for them, and re-layouts  31.2 us (1%)
    dot_general x35, matrix products, mm(): return lax.dot_general(lhs, rhs, dims, preferred_element_type=F32)  710 us
    ppermute x7, waiting for transfers between devices, across(): return lax.ppermute(v, 'tp', chip_pairs)  672 us
    pallas_call x8, Pallas kernels, sum_rows(): pl.pallas_call(functools.partial(sum_kernel, tuple(terms), n_in, len(adds...  573 us
    pallas_call x8, Pallas kernels, mlp_chunk(): pl.pallas_call(functools.partial(mlp_kernel, min(256, tn)), grid=(cols //...  515 us
    reduce_scatter x14, waiting for transfers between devices, weight_grad(): lax.psum_scatter(part, 'dp', scatter_dimension=axis, tiled=True)  123 us
    pallas_call x2, Pallas kernels, attention(): pl.pallas_call(functools.partial(attention_kernel, head_dim ** (-0.5)), g...  97.9 us
  transfers between devices with their start and end apart: 45, of which 8 were waited for; matrix products, arithmetic and copies ran while one was open for 26% of the time, Pallas kernels for 39%

profile of v1, /device:TPU:0, one launch (start us, length us, event | category | flops | bytes accessed | tf_op | source)
XLA Modules:
  0.0 2944.6 jit_solution(5049220084952809623)
XLA Ops:
  26.4 12.4 fusion
  47.4 179.2 %collective-permute-done.2.first_ref = bf16[2048,2048]{1,0:T(8,128)(2,1)} collective-permute-done((bf16[2048,2048]{1,0:T(8,128)(2,1)}, bf16[2048,2048]{1,0:T(8,128)(2,1)}, u32[]{:S(2)}, u32[]{:S(2)}) %collective-permute-start.2) | collective-permute-done | bytes 8388640 | tf_op jit(solution)/shard_map/ppermute | solution.py:272
  226.7 14.3 pair.4.h_ref
  241.0 14.4 convolution_convert_fusion.4.key_ref.val_ref
  255.4 14.3 pair.5.gy_ref
  269.7 15.5 convolution_convert_fusion.5.q_ref
  285.2 14.6 convolution_convert_fusion.3.do_ref
  299.8 48.9 %attention.2 = (bf16[4096,512]{1,0:T(8,128)(2,1)}, bf16[4096,512]{1,0:T(8,128)(2,1)}, f32[4096,512]{1,0:T(8,128)}) custom-call(s32[1024,1]{1,0:T(8,128)} %copy.26.pos_q_ref, s32[1,1024]{1,0:T(1,128)} %bitcast.83, bf16[4096,512]{1,0:T(8,128)(2,1)} %convolution_convert_fusion.5.q_ref, bf16[4096,512]{1,0:T(8,128)(2,1)} %convolution_convert_fusion.4.key_ref.val_ref, ...), custom_call_target="tpu_custom_call" | custom-call | flops 42949672960 | bytes 29360128 | tf_op jit(solution)/shard_map/attention/pallas_call | solution.py:98
  353.9 51.7 %collective-permute-done.4.first_ref = bf16[2048,2048]{1,0:T(8,128)(2,1)} collective-permute-done((bf16[2048,2048]{1,0:T(8,128)(2,1)}, bf16[2048,2048]{1,0:T(8,128)(2,1)}, u32[]{:S(2)}, u32[]{:S(2)}) %collective-permute-start.4) | collective-permute-done | bytes 8388640 | tf_op jit(solution)/shard_map/ppermute | solution.py:272
  405.6 64.3 %mlp_chunk.8 = (bf16[4096,1024]{1,0:T(8,128)(2,1)}, bf16[4096,1024]{1,0:T(8,128)(2,1)}, bf16[4096,1024]{1,0:T(8,128)(2,1)}) custom-call(bf16[4096,2048]{1,0:T(8,128)(2,1)} %pair.4.h_ref, bf16[4096,2048]{1,0:T(8,128)(2,1)} %pair.5.gy_ref, bf16[2,2048,1024]{2,1,0:T(8,128)(2,1)} %all-gather.12.cloned.1.call-done.win_ref.refs_2_, ...), custom_call_target="tpu_custom_call" | custom-call | flops 51539607552 | bytes 92274688 | tf_op jit(solution)/shard_map/mlp_chunk/pallas_call | solution.py:140
  469.9 14.4 pair.6.h_ref
  484.4 16.2 convolution_convert_fusion.1.key_ref.val_ref
  511.0 14.5 pair.7.gy_ref
  525.5 14.3 convolution_convert_fusion.do_ref
  539.7 48.9 %attention.3 = (bf16[4096,512]{1,0:T(8,128)(2,1)}, bf16[4096,512]{1,0:T(8,128)(2,1)}, f32[4096,512]{1,0:T(8,128)}) custom-call(s32[1024,1]{1,0:T(8,128)} %copy.26.pos_q_ref, s32[1,1024]{1,0:T(1,128)} %bitcast.84, bf16[4096,512]{1,0:T(8,128)(2,1)} %convolution_convert_fusion.2.q_ref, bf16[4096,512]{1,0:T(8,128)(2,1)} %convolution_convert_fusion.1.key_ref.val_ref, ...), custom_call_target="tpu_custom_call" | custom-call | flops 42949672960 | bytes 29360128 | tf_op jit(solution)/shard_map/attention/pallas_call | solution.py:98
  588.7 65.2 %mlp_chunk.9 = (bf16[4096,1024]{1,0:T(8,128)(2,1)}, bf16[4096,1024]{1,0:T(8,128)(2,1)}, bf16[4096,1024]{1,0:T(8,128)(2,1)}) custom-call(bf16[4096,2048]{1,0:T(8,128)(2,1)} %pair.6.h_ref, bf16[4096,2048]{1,0:T(8,128)(2,1)} %pair.7.gy_ref, bf16[2,2048,1024]{2,1,0:T(8,128)(2,1)} %all-gather.12.cloned.1.call-done.win_ref.refs_2_, ...), custom_call_target="tpu_custom_call" | custom-call | flops 51539607552 | bytes 92274688 | tf_op jit(solution)/shard_map/mlp_chunk/pallas_call | solution.py:140
  653.9 13.1 fusion.2
  667.0 13.9 convolution_add_fusion.13
  686.4 14.5 fusion.3
  700.9 12.2 convolution_add_fusion.12
  721.6 24.9 fusion.4
  746.5 21.7 convolution_add_fusion.3
  768.2 44.5 %collective-permute-done.8 = f32[2048,512]{1,0:T(8,128)} collective-permute-done((f32[2048,512]{1,0:T(8,128)}, f32[2048,512]{1,0:T(8,128)}, u32[]{:S(2)}, u32[]{:S(2)}) %collective-permute-start.8) | collective-permute-done | bytes 4194336 | tf_op jit(solution)/shard_map/ppermute | solution.py:272
  829.5 24.4 fusion.6
  853.9 22.7 convolution_add_fusion.11
  876.6 22.7 fusion.7
  899.3 24.1 convolution_add_fusion.10.rest_0_
  923.4 64.4 %mlp_chunk.10 = (bf16[4096,1024]{1,0:T(8,128)(2,1)}, bf16[4096,1024]{1,0:T(8,128)(2,1)}, bf16[4096,1024]{1,0:T(8,128)(2,1)}) custom-call(bf16[4096,2048]{1,0:T(8,128)(2,1)} %pair.4.h_ref, bf16[4096,2048]{1,0:T(8,128)(2,1)} %pair.5.gy_ref, bf16[2,2048,1024]{2,1,0:T(8,128)(2,1)} %all-gather.22.cloned.1.call-done.win_ref.refs_5_, ...), custom_call_target="tpu_custom_call" | custom-call | flops 51539607552 | bytes 92274688 | tf_op jit(solution)/shard_map/mlp_chunk/pallas_call | solution.py:140
  987.8 64.2 %mlp_chunk.11 = (bf16[4096,1024]{1,0:T(8,128)(2,1)}, bf16[4096,1024]{1,0:T(8,128)(2,1)}, bf16[4096,1024]{1,0:T(8,128)(2,1)}) custom-call(bf16[4096,2048]{1,0:T(8,128)(2,1)} %pair.6.h_ref, bf16[4096,2048]{1,0:T(8,128)(2,1)} %pair.7.gy_ref, bf16[2,2048,1024]{2,1,0:T(8,128)(2,1)} %all-gather.22.cloned.1.call-done.win_ref.refs_5_, ...), custom_call_target="tpu_custom_call" | custom-call | flops 51539607552 | bytes 92274688 | tf_op jit(solution)/shard_map/mlp_chunk/pallas_call | solution.py:140
  1052.0 22.6 fusion.8
  1074.5 22.2 convolution_add_fusion.2.rest_0_
  1096.8 64.2 %mlp_chunk.12 = (bf16[4096,1024]{1,0:T(8,128)(2,1)}, bf16[4096,1024]{1,0:T(8,128)(2,1)}, bf16[4096,1024]{1,0:T(8,128)(2,1)}) custom-call(bf16[4096,2048]{1,0:T(8,128)(2,1)} %pair.4.h_ref, bf16[4096,2048]{1,0:T(8,128)(2,1)} %pair.5.gy_ref, bf16[2,2048,1024]{2,1,0:T(8,128)(2,1)} %all-gather.26.cloned.1.call-done.win_ref.refs_8_, ...), custom_call_target="tpu_custom_call" | custom-call | flops 51539607552 | bytes 92274688 | tf_op jit(solution)/shard_map/mlp_chunk/pallas_call | solution.py:140
  1161.0 64.2 %mlp_chunk.13 = (bf16[4096,1024]{1,0:T(8,128)(2,1)}, bf16[4096,1024]{1,0:T(8,128)(2,1)}, bf16[4096,1024]{1,0:T(8,128)(2,1)}) custom-call(bf16[4096,2048]{1,0:T(8,128)(2,1)} %pair.6.h_ref, bf16[4096,2048]{1,0:T(8,128)(2,1)} %pair.7.gy_ref, bf16[2,2048,1024]{2,1,0:T(8,128)(2,1)} %all-gather.26.cloned.1.call-done.win_ref.refs_8_, ...), custom_call_target="tpu_custom_call" | custom-call | flops 51539607552 | bytes 92274688 | tf_op jit(solution)/shard_map/mlp_chunk/pallas_call | solution.py:140
  1225.1 22.8 fusion.9
  1247.9 24.1 convolution_add_fusion.9
  1272.0 22.9 fusion.10
  1294.9 24.1 convolution_add_fusion.8.rest_0_
  1319.1 64.3 %mlp_chunk.14 = (bf16[4096,1024]{1,0:T(8,128)(2,1)}, bf16[4096,1024]{1,0:T(8,128)(2,1)}, bf16[4096,1024]{1,0:T(8,128)(2,1)}) custom-call(bf16[4096,2048]{1,0:T(8,128)(2,1)} %pair.4.h_ref, bf16[4096,2048]{1,0:T(8,128)(2,1)} %pair.5.gy_ref, bf16[2,2048,1024]{2,1,0:T(8,128)(2,1)} %all-gather.30.cloned.1.call-done.win_ref.refs_11_, ...), custom_call_target="tpu_custom_call" | custom-call | flops 51539607552 | bytes 92274688 | tf_op jit(solution)/shard_map/mlp_chunk/pallas_call | solution.py:140
  1383.3 64.7 %mlp_chunk.15 = (bf16[4096,1024]{1,0:T(8,128)(2,1)}, bf16[4096,1024]{1,0:T(8,128)(2,1)}, bf16[4096,1024]{1,0:T(8,128)(2,1)}) custom-call(bf16[4096,2048]{1,0:T(8,128)(2,1)} %pair.6.h_ref, bf16[4096,2048]{1,0:T(8,128)(2,1)} %pair.7.gy_ref, bf16[2,2048,1024]{2,1,0:T(8,128)(2,1)} %all-gather.30.cloned.1.call-done.win_ref.refs_11_, ...), custom_call_target="tpu_custom_call" | custom-call | flops 51539607552 | bytes 92274688 | tf_op jit(solution)/shard_map/mlp_chunk/pallas_call | solution.py:140
  1448.0 47.7 %shard_map.145 = f32[2048,2048]{1,0:T(8,128)} custom-call(bf16[4096,1024]{1,0:T(8,128)(2,1)} %get-tuple-element.82.refs_0_, bf16[1024,2048]{1,0:T(8,128)(2,1)} %all-gather.14.cloned.1.call-done.wout_ref.refs_1_, bf16[4096,1024]{1,0:T(8,128)(2,1)} %get-tuple-element.97.refs_2_, bf16[1024,2048]{1,0:T(8,128)(2,1)} %all-gather.24.cloned.1.call-done.wout_ref.refs_3_, ...), custom_call_target="tpu_custom_call" | custom-call | flops 38654705664 | bytes 73400320 | tf_op jit(solution)/shard_map/pallas_call | solution.py:196
  1497.6 24.3 fusion.11
  1524.2 21.9 convolution_add_fusion.1.refs_11_
  1556.6 24.8 collective-permute-done.9.refs_10_
  1581.4 50.4 %shard_map.146 = f32[2048,2048]{1,0:T(8,128)} custom-call(bf16[4096,1024]{1,0:T(8,128)(2,1)} %get-tuple-element.82.refs_0_, bf16[1024,2048]{1,0:T(8,128)(2,1)} %all-gather.14.cloned.1.call-done.wout_ref.refs_1_, bf16[4096,1024]{1,0:T(8,128)(2,1)} %get-tuple-element.97.refs_2_, bf16[1024,2048]{1,0:T(8,128)(2,1)} %all-gather.24.cloned.1.call-done.wout_ref.refs_3_, ...), custom_call_target="tpu_custom_call" | custom-call | flops 38654705664 | bytes 90177536 | tf_op jit(solution)/shard_map/pallas_call | solution.py:196
  1631.8 22.7 fusion.12
  1654.4 24.3 convolution_add_fusion.7
  1678.8 22.9 fusion.13
  1701.7 24.3 convolution_add_fusion.6.refs_14_
  1726.1 92.1 %shard_map.147 = f32[2048,2048]{1,0:T(8,128)} custom-call(bf16[4096,1024]{1,0:T(8,128)(2,1)} %get-tuple-element.89.refs_0_, bf16[4096,1024]{1,0:T(8,128)(2,1)} %get-tuple-element.93.refs_1_, bf16[2,2048,1024]{2,1,0:T(8,128)(2,1)} %all-gather.12.cloned.1.call-done.win_ref.refs_2_, bf16[4096,1024]{1,0:T(8,128)(2,1)} %get-tuple-element.103.refs_3_, ...), custom_call_target="tpu_custom_call" | custom-call | flops 73014444032 | bytes 195035136 | tf_op jit(solution)/shard_map/pallas_call | solution.py:196
  1818.2 22.7 fusion.14
  1840.9 24.3 convolution_add_fusion.refs_15_
  1867.0 93.3 %shard_map.148 = f32[2048,2048]{1,0:T(8,128)} custom-call(bf16[4096,1024]{1,0:T(8,128)(2,1)} %get-tuple-element.89.refs_0_, bf16[4096,1024]{1,0:T(8,128)(2,1)} %get-tuple-element.93.refs_1_, bf16[2,2048,1024]{2,1,0:T(8,128)(2,1)} %all-gather.12.cloned.1.call-done.win_ref.refs_2_, bf16[4096,1024]{1,0:T(8,128)(2,1)} %get-tuple-element.103.refs_3_, ...), custom_call_target="tpu_custom_call" | custom-call | flops 73014444032 | bytes 211812352 | tf_op jit(solution)/shard_map/pallas_call | solution.py:196
  1960.3 22.7 fusion.15
  1982.9 24.1 convolution_add_fusion.5
  2007.1 22.9 fusion.16
  2030.0 24.3 convolution_add_fusion.4.refs_10_
  2054.2 49.2 %shard_map.149.refs_14_ = f32[2048,2048]{1,0:T(8,128)} custom-call(bf16[4096,1024]{1,0:T(8,128)(2,1)} %get-tuple-element.81.rest_0_.refs_0_, bf16[1024,2048]{1,0:T(8,128)(2,1)} %all-gather.14.cloned.1.call-done.wout_ref.refs_1_, bf16[4096,1024]{1,0:T(8,128)(2,1)} %get-tuple-element.96.rest_0_.refs_2_, ...), custom_call_target="tpu_custom_call" | custom-call | flops 38654705664 | bytes 73400320 | tf_op jit(solution)/shard_map/pallas_call | solution.py:196
  2103.6 91.8 %shard_map.150.refs_12_ = f32[2048,2048]{1,0:T(8,128)} custom-call(bf16[4096,1024]{1,0:T(8,128)(2,1)} %get-tuple-element.87.refs_0_, bf16[4096,1024]{1,0:T(8,128)(2,1)} %get-tuple-element.91.refs_1_, bf16[2,2048,1024]{2,1,0:T(8,128)(2,1)} %all-gather.12.cloned.1.call-done.win_ref.refs_2_, bf16[4096,1024]{1,0:T(8,128)(2,1)} %get-tuple-element.101.refs_3_, ...), custom_call_target="tpu_custom_call" | custom-call | flops 73014444032 | bytes 195035136 | tf_op jit(solution)/shard_map/pallas_call | solution.py:196
  2199.0 393.9 %collective-permute-done.17 = bf16[1024,128]{1,0:T(8,128)(2,1)S(1)} collective-permute-done((bf16[1024,128]{1,0:T(8,128)(2,1)S(1)}, bf16[1024,128]{1,0:T(8,128)(2,1)S(1)}, u32[]{:S(2)}, u32[]{:S(2)}) %collective-permute-start.17) | collective-permute-done | bytes 262176 | tf_op jit(solution)/shard_map/ppermute | solution.py:272
  2638.1 27.5 reduce-scatter.38.cloned.1.call-done.piece_ref
  2669.8 95.2 %reduce-scatter.24.cloned.1.call-done.piece_ref = f32[1024,1024]{1,0:T(8,128)} async-done(((f32[2048,1024]{1,0:T(8,128)}), f32[1024,1024]{1,0:T(8,128)}) %reduce-scatter.24.cloned.1.call-update) | async-done | bytes 4194320 | tf_op jit(solution)/shard_map/reduce_scatter | solution.py:323
  2769.2 50.9 %shard_map.151.refs_18_ = bf16[2048,2048]{1,0:T(8,128)(2,1)} custom-call(bf16[4096,1024]{1,0:T(8,128)(2,1)} %get-tuple-element.81.rest_0_.refs_0_, bf16[1024,2048]{1,0:T(8,128)(2,1)} %all-gather.14.cloned.1.call-done.wout_ref.refs_1_, bf16[4096,1024]{1,0:T(8,128)(2,1)} %get-tuple-element.96.rest_0_.refs_2_, ...), custom_call_target="tpu_custom_call" | custom-call | flops 38654705664 | bytes 106954752 | tf_op jit(solution)/shard_map/pallas_call | solution.py:196
  2820.1 97.5 %shard_map.152.dh_ref = bf16[2048,2048]{1,0:T(8,128)(2,1)} custom-call(bf16[4096,1024]{1,0:T(8,128)(2,1)} %get-tuple-element.87.refs_0_, bf16[4096,1024]{1,0:T(8,128)(2,1)} %get-tuple-element.91.refs_1_, bf16[2,2048,1024]{2,1,0:T(8,128)(2,1)} %all-gather.12.cloned.1.call-done.win_ref.refs_2_, bf16[4096,1024]{1,0:T(8,128)(2,1)} %get-tuple-element.101.refs_3_, ...), custom_call_target="tpu_custom_call" | custom-call | flops 77309411328 | bytes 239075328 | tf_op jit(solution)/shard_map/pallas_call | solution.py:196
  2917.6 15.7 shard_map.153
  (207 shorter events, 152.0 us)
Async XLA Ops:
  7.2 233.8 %all-gather.18.cloned.1.call-start = ((), (), s32[]{:S(2)}) async-start(), calls=%async_computation.18 | async-start | bytes 3145728 | tf_op jit(solution)/shard_map/all_gather | solution.py:291
  7.9 261.8 %all-gather.16.cloned.1.call-start = ((), (), s32[]{:S(2)}) async-start(), calls=%async_computation.17 | async-start | bytes 3145728 | tf_op jit(solution)/shard_map/all_gather | solution.py:292
  8.6 276.5 %all-gather.20.cloned.1.call-start = ((), (), s32[]{:S(2)}) async-start(), calls=%async_computation.19 | async-start | bytes 3145728 | tf_op jit(solution)/shard_map/all_gather | solution.py:293
  9.4 396.2 %all-gather.14.cloned.1.call-start = ((), (), s32[]{:S(2)}) async-start(), calls=%async_computation.16 | async-start | bytes 6291456 | tf_op jit(solution)/shard_map/all_gather | solution.py:298
  26.4 379.2 %all-gather.12.cloned.1.call-start = ((), (), s32[]{:S(2)}) async-start(), calls=%async_computation.15 | async-start | bytes 12582912 | tf_op jit(solution)/shard_map/all_gather | solution.py:297
  38.8 884.6 %all-gather.24.cloned.1.call-start = ((), (), s32[]{:S(2)}) async-start(), calls=%async_computation.21 | async-start | bytes 6291456 | tf_op jit(solution)/shard_map/all_gather | solution.py:298
  39.4 884.0 %all-gather.22.cloned.1.call-start = ((), (), s32[]{:S(2)}) async-start(), calls=%async_computation.20 | async-start | bytes 12582912 | tf_op jit(solution)/shard_map/all_gather | solution.py:297
  40.1 1056.7 %all-gather.28.cloned.1.call-start = ((), (), s32[]{:S(2)}) async-start(), calls=%async_computation.23 | async-start | bytes 6291456 | tf_op jit(solution)/shard_map/all_gather | solution.py:298
  40.9 1055.9 %all-gather.26.cloned.1.call-start = ((), (), s32[]{:S(2)}) async-start(), calls=%async_computation.22 | async-start | bytes 12582912 | tf_op jit(solution)/shard_map/all_gather | solution.py:297
  41.6 1277.5 %all-gather.32.cloned.1.call-start = ((), (), s32[]{:S(2)}) async-start(), calls=%async_computation.25 | async-start | bytes 6291456 | tf_op jit(solution)/shard_map/all_gather | solution.py:298
  41.6 185.0 %collective-permute-start.2 = (bf16[2048,2048]{1,0:T(8,128)(2,1)}, bf16[2048,2048]{1,0:T(8,128)(2,1)}, u32[]{:S(2)}, u32[]{:S(2)}) collective-permute-start(bf16[2048,2048]{1,0:T(8,128)(2,1)} %shard_map.144.first_ref), channel_id=1, source_target_pairs={{0,2},{1,3},{2,0},{3,1},{4,6},{5,7},{6,4},{7,5}} | collective-permute-start | bytes 25165832 | tf_op jit(solution)/shard_map/ppermute | solution.py:272
  45.0 181.6 %collective-permute-start = (bf16[2048,2048]{1,0:T(8,128)(2,1)}, bf16[2048,2048]{1,0:T(8,128)(2,1)}, u32[]{:S(2)}, u32[]{:S(2)}) collective-permute-start(bf16[2048,2048]{1,0:T(8,128)(2,1)} %shard_map.144.first_ref), channel_id=1, source_target_pairs={{0,1},{1,0},{2,3},{3,2},{4,5},{5,4},{6,7},{7,6}} | collective-permute-start | bytes 25165832 | tf_op jit(solution)/shard_map/ppermute | solution.py:269
  45.1 210.3 %collective-permute-start.1 = (bf16[2048,2048]{1,0:T(8,128)(2,1)}, bf16[2048,2048]{1,0:T(8,128)(2,1)}, u32[]{:S(2)}, u32[]{:S(2)}) collective-permute-start(bf16[2048,2048]{1,0:T(8,128)(2,1)} %first_ref.1), channel_id=1, source_target_pairs={{0,1},{1,0},{2,3},{3,2},{4,5},{5,4},{6,7},{7,6}} | collective-permute-start | bytes 25165832 | tf_op jit(solution)/shard_map/ppermute | solution.py:269
  45.6 1273.5 %all-gather.30.cloned.1.call-start = ((), (), s32[]{:S(2)}) async-start(), calls=%async_computation.24 | async-start | bytes 12582912 | tf_op jit(solution)/shard_map/all_gather | solution.py:297
  45.6 360.0 %collective-permute-start.4 = (bf16[2048,2048]{1,0:T(8,128)(2,1)}, bf16[2048,2048]{1,0:T(8,128)(2,1)}, u32[]{:S(2)}, u32[]{:S(2)}) collective-permute-start(bf16[2048,2048]{1,0:T(8,128)(2,1)} %first_ref.1), channel_id=1, source_target_pairs={{0,2},{1,3},{2,0},{3,1},{4,6},{5,7},{6,4},{7,5}} | collective-permute-start | bytes 25165832 | tf_op jit(solution)/shard_map/ppermute | solution.py:272
  46.3 2149.6 %reduce-scatter.18.cloned.1.call-start = ((), (), s32[]{:S(2)}) async-start(), calls=%async_computation.27 | async-start | bytes 1572864 | tf_op jit(solution)/shard_map/reduce_scatter | solution.py:369
  226.7 243.3 %collective-permute-start.3 = (bf16[2048,2048]{1,0:T(8,128)(2,1)}, bf16[2048,2048]{1,0:T(8,128)(2,1)}, u32[]{:S(2)}, u32[]{:S(2)}) collective-permute-start(bf16[2048,2048]{1,0:T(8,128)(2,1)} %collective-permute-done.2.first_ref), channel_id=1, source_target_pairs={{0,1},{1,0},{2,3},{3,2},{4,5},{5,4},{6,7},{7,6}} | collective-permute-start | bytes 25165832 | tf_op jit(solution)/shard_map/ppermute | solution.py:269
  353.4 414.7 %collective-permute-start.6 = (f32[2048,512]{1,0:T(8,128)}, f32[2048,512]{1,0:T(8,128)}, u32[]{:S(2)}, u32[]{:S(2)}) collective-permute-start(f32[2048,512]{1,0:T(8,128)} %slice.41), channel_id=1, source_target_pairs={{0,1},{1,0},{2,3},{3,2},{4,5},{5,4},{6,7},{7,6}} | collective-permute-start | bytes 12582920 | tf_op jit(solution)/shard_map/ppermute | solution.py:269
  405.6 105.4 %collective-permute-start.5 = (bf16[2048,2048]{1,0:T(8,128)(2,1)}, bf16[2048,2048]{1,0:T(8,128)(2,1)}, u32[]{:S(2)}, u32[]{:S(2)}) collective-permute-start(bf16[2048,2048]{1,0:T(8,128)(2,1)} %collective-permute-done.4.first_ref), channel_id=1, source_target_pairs={{0,1},{1,0},{2,3},{3,2},{4,5},{5,4},{6,7},{7,6}} | collective-permute-start | bytes 25165832 | tf_op jit(solution)/shard_map/ppermute | solution.py:269
  484.4 16.2 copy-start
  484.4 16.2 copy-start.5
  680.9 20.0 slice-start.4
  685.9 27.3 collective-permute-start.7
  713.1 33.3 %slice-start.8 = ((s8[16777216]{0:T(1024)(128)(4,1)}), s8[4194304]{0:T(1024)(128)(4,1)S(1)}, s32[]{:S(2)}) async-start(s8[16777216]{0:T(1024)(128)(4,1)} %bitcast.77), calls=%async_computation.49 | async-start | bytes 8388608
  713.1 33.3 %slice-start.18 = ((s8[8388608]{0:T(1024)(128)(4,1)}), s8[4194304]{0:T(1024)(128)(4,1)S(1)}, s32[]{:S(2)}) async-start(s8[8388608]{0:T(1024)(128)(4,1)} %bitcast.88), calls=%async_computation.59 | async-start | bytes 8388608
  719.9 26.6 slice-start.9
  719.9 26.6 slice-start.10
  719.9 26.6 slice-start.11
  719.9 26.6 slice-start.19
  719.9 92.8 %collective-permute-start.8 = (f32[2048,512]{1,0:T(8,128)}, f32[2048,512]{1,0:T(8,128)}, u32[]{:S(2)}, u32[]{:S(2)}) collective-permute-start(f32[2048,512]{1,0:T(8,128)} %slice_add_fusion), channel_id=1, source_target_pairs={{0,2},{1,3},{2,0},{3,1},{4,6},{5,7},{6,4},{7,5}} | collective-permute-start | bytes 12582920 | tf_op jit(solution)/shard_map/ppermute | solution.py:272
  812.7 16.8 slice-start
  812.7 16.8 slice-start.1
  818.8 35.1 %slice-start.16 = ((s8[8388608]{0:T(1024)(128)(4,1)}), s8[4194304]{0:T(1024)(128)(4,1)S(1)}, s32[]{:S(2)}) async-start(s8[8388608]{0:T(1024)(128)(4,1)} %bitcast.86), calls=%async_computation.57 | async-start | bytes 8388608
  829.5 24.4 slice-start.17
  1052.0 22.6 copy-start.9
  1495.6 28.5 slice-start.12
  1497.5 24.4 copy-start.1
  1497.5 26.6 slice-start.13
  1497.5 26.6 slice-start.14
  1497.6 26.6 slice-start.15
  1497.6 24.3 collective-permute-start.15
  1522.4 26.1 collective-permute-start.16
  1550.9 1042.3 %reduce-scatter.16.cloned.1.call-start = ((), (), s32[]{:S(2)}) async-start(), calls=%async_computation.26 | async-start | bytes 6291456 | tf_op jit(solution)/shard_map/reduce_scatter | solution.py:323
  1551.6 1044.3 %reduce-scatter.20.cloned.1.call-start = ((), (), s32[]{:S(2)}) async-start(), calls=%async_computation.28 | async-start | bytes 6291456 | tf_op jit(solution)/shard_map/reduce_scatter | solution.py:323
  1552.2 1047.7 %reduce-scatter.44.cloned.1.call-start = ((), (), s32[]{:S(2)}) async-start(), calls=%async_computation.40 | async-start | bytes 12582912 | tf_op jit(solution)/shard_map/reduce_scatter | solution.py:323
  1552.8 1051.3 %reduce-scatter.36.cloned.1.call-start = ((), (), s32[]{:S(2)}) async-start(), calls=%async_computation.36 | async-start | bytes 12582912 | tf_op jit(solution)/shard_map/reduce_scatter | solution.py:323
  1553.3 1055.0 %reduce-scatter.34.cloned.1.call-start = ((), (), s32[]{:S(2)}) async-start(), calls=%async_computation.35 | async-start | bytes 12582912 | tf_op jit(solution)/shard_map/reduce_scatter | solution.py:323
  1553.9 1058.6 %reduce-scatter.42.cloned.1.call-start = ((), (), s32[]{:S(2)}) async-start(), calls=%async_computation.39 | async-start | bytes 12582912 | tf_op jit(solution)/shard_map/reduce_scatter | solution.py:323
  1554.5 1062.4 %reduce-scatter.32.cloned.1.call-start = ((), (), s32[]{:S(2)}) async-start(), calls=%async_computation.34 | async-start | bytes 12582912 | tf_op jit(solution)/shard_map/reduce_scatter | solution.py:323
  1555.3 1065.8 %reduce-scatter.30.cloned.1.call-start = ((), (), s32[]{:S(2)}) async-start(), calls=%async_computation.33 | async-start | bytes 12582912 | tf_op jit(solution)/shard_map/reduce_scatter | solution.py:323
  1555.8 1069.5 %reduce-scatter.40.cloned.1.call-start = ((), (), s32[]{:S(2)}) async-start(), calls=%async_computation.38 | async-start | bytes 12582912 | tf_op jit(solution)/shard_map/reduce_scatter | solution.py:323
  1555.9 25.5 collective-permute-start.9
  1556.6 1073.0 %reduce-scatter.28.cloned.1.call-start = ((), (), s32[]{:S(2)}) async-start(), calls=%async_computation.32 | async-start | bytes 12582912 | tf_op jit(solution)/shard_map/reduce_scatter | solution.py:323
  1678.8 955.1 %reduce-scatter.26.cloned.1.call-start = ((), (), s32[]{:S(2)}) async-start(), calls=%async_computation.31 | async-start | bytes 12582912 | tf_op jit(solution)/shard_map/reduce_scatter | solution.py:323
  1726.1 939.5 %reduce-scatter.38.cloned.1.call-start = ((), (), s32[]{:S(2)}) async-start(), calls=%async_computation.37 | async-start | bytes 12582912 | tf_op jit(solution)/shard_map/reduce_scatter | solution.py:323
  1818.2 48.8 %collective-permute-start.10 = (f32[2048,2048]{1,0:T(8,128)}, f32[2048,2048]{1,0:T(8,128)}, u32[]{:S(2)}, u32[]{:S(2)}) collective-permute-start(f32[2048,2048]{1,0:T(8,128)} %shard_map.147), channel_id=1, source_target_pairs={{0,1},{1,0},{2,3},{3,2},{4,5},{5,4},{6,7},{7,6}} | collective-permute-start | bytes 50331656 | tf_op jit(solution)/shard_map/ppermute | solution.py:269
  1865.2 899.7 %reduce-scatter.24.cloned.1.call-start = ((), (), s32[]{:S(2)}) async-start(), calls=%async_computation.30 | async-start | bytes 12582912 | tf_op jit(solution)/shard_map/reduce_scatter | solution.py:323
  1865.3 903.9 %collective-permute-start.12 = (f32[2048,2048]{1,0:T(8,128)}, f32[2048,2048]{1,0:T(8,128)}, u32[]{:S(2)}, u32[]{:S(2)}) collective-permute-start(f32[2048,2048]{1,0:T(8,128)} %shard_map.146), channel_id=1, source_target_pairs={{0,2},{1,3},{2,0},{3,1},{4,6},{5,7},{6,4},{7,5}} | collective-permute-start | bytes 50331656 | tf_op jit(solution)/shard_map/ppermute | solution.py:272
  2007.0 926.3 %reduce-scatter.22.cloned.1.call-start = ((), (), s32[]{:S(2)}) async-start(), calls=%async_computation.29 | async-start | bytes 12582912 | tf_op jit(solution)/shard_map/reduce_scatter | solution.py:323
  2103.4 665.8 %collective-permute-start.11 = (f32[2048,2048]{1,0:T(8,128)}, f32[2048,2048]{1,0:T(8,128)}, u32[]{:S(2)}, u32[]{:S(2)}) collective-permute-start(f32[2048,2048]{1,0:T(8,128)} %shard_map.149.refs_14_), channel_id=1, source_target_pairs={{0,1},{1,0},{2,3},{3,2},{4,5},{5,4},{6,7},{7,6}} | collective-permute-start | bytes 50331656 | tf_op jit(solution)/shard_map/ppermute | solution.py:269
  2195.5 624.6 %collective-permute-start.13 = (f32[2048,2048]{1,0:T(8,128)}, f32[2048,2048]{1,0:T(8,128)}, u32[]{:S(2)}, u32[]{:S(2)}) collective-permute-start(f32[2048,2048]{1,0:T(8,128)} %shard_map.150.refs_12_), channel_id=1, source_target_pairs={{0,1},{1,0},{2,3},{3,2},{4,5},{5,4},{6,7},{7,6}} | collective-permute-start | bytes 50331656 | tf_op jit(solution)/shard_map/ppermute | solution.py:269
  2195.9 624.2 %collective-permute-start.14 = (f32[2048,2048]{1,0:T(8,128)}, f32[2048,2048]{1,0:T(8,128)}, u32[]{:S(2)}, u32[]{:S(2)}) collective-permute-start(f32[2048,2048]{1,0:T(8,128)} %shard_map.148), channel_id=1, source_target_pairs={{0,2},{1,3},{2,0},{3,1},{4,6},{5,7},{6,4},{7,5}} | collective-permute-start | bytes 50331656 | tf_op jit(solution)/shard_map/ppermute | solution.py:272
  2197.0 395.9 %collective-permute-start.17 = (bf16[1024,128]{1,0:T(8,128)(2,1)S(1)}, bf16[1024,128]{1,0:T(8,128)(2,1)S(1)}, u32[]{:S(2)}, u32[]{:S(2)}) collective-permute-start(bf16[1024,128]{1,0:T(8,128)(2,1)S(1)} %convert_element_type.38), channel_id=1, source_target_pairs={{0,2},{1,3},{2,0},{3,1},{4,6},{5,7},{6,4},{7,5}} | collective-permute-start | bytes 786440 | tf_op jit(solution)/shard_map/ppermute | solution.py:272
  2593.1 5.5 collective-permute-start.18
  (12 other events, 146.6 us)
Sparse Core Ops, SparseCore 0:
  9.5 33.0 all-gather.17
  44.1 30.2 all-gather.15
  76.0 30.2 all-gather.19
  107.7 53.9 all-gather.13
  163.6 101.1 all-gather.11
  266.2 53.9 all-gather.23
  321.7 101.1 all-gather.21
  424.4 53.9 all-gather.27
  479.9 101.1 all-gather.25
  582.5 53.9 all-gather.31
  638.0 101.1 all-gather.29
  1551.0 18.8 reduce-scatter.17
  1572.2 51.5 reduce-scatter.15
  1625.9 51.5 reduce-scatter.19
  1679.7 96.5 reduce-scatter.43
  1778.4 96.5 reduce-scatter.35
  1877.6 96.5 reduce-scatter.33
  1976.3 96.5 reduce-scatter.41
  2075.2 96.5 reduce-scatter.31
  2173.9 96.5 reduce-scatter.29
  2272.7 96.5 reduce-scatter.39
  2371.5 96.5 reduce-scatter.27
  2470.3 96.5 reduce-scatter.25
  2569.0 96.5 reduce-scatter.37
  2668.4 96.5 reduce-scatter.23
  2767.1 96.5 reduce-scatter.21
